TPU v7x, 32 devices: a whole 2x2x4 slice. The times are simulated.
32 devices in a mesh: ens: 2 (over y), box: 4 (over z), slab: 4 (over x, core).
Axes of the slice: x: 2, y: 2, z: 4, core: 2. Of those that a mesh axis runs over, the one named last changes fastest.
Arguments:
- pressure_now: float32 [4, 64, 64, 256], P('ens', 'box', 'slab'), parts along dimension 0, may hold values from -6 to 6
- pressure_prev: float32 [4, 64, 64, 256], P('ens', 'box', 'slab'), parts along dimension 0, may hold values from -6 to 6
- courant_sq: float32 [64, 64, 256], P('box', 'slab'), may hold values from 0.04 to 0.28
- member_profiles: float32 [8, 64], replicated, may hold values from -0.15 to 0.15
- member_ids: int32 [4], P('ens'), parts along dimension 0, may hold values from 0 to 7, as said below
- stored_slabs: float32 [8, 16, 6144], P('slab'), may hold values from -6 to 6
- slab_home: int32 [2], P('ens'), parts along dimension 0, may hold values from 0 to 7
- interp_weights: float32 [2, 16], replicated, may hold values from -1.5 to 1.5
- surface_cells: int32 [6, 1024], replicated, may hold values from 0 to 1048575, as said below
Outputs:
- pressure_next: float32 [4, 64, 64, 256], P('ens', 'box', 'slab'), parts along dimension 0
- pressure_last: float32 [4, 64, 64, 256], P('ens', 'box', 'slab'), parts along dimension 0
There are 2 independent parts, one for each index of `ens`. A program takes and returns all parts, laid end to end along the dimension named above; an argument that names none is the same for every part. Nothing has to cross between parts.
Inputs may be any that keep to these rules, and one draw needn't show every extreme that they name: `surface_cells`: row f lists 1024 cells, flat index (x 64 + z) * 256 + y, on one face of the box surface 0 cells inside the grid: x low, x high, z low, z high, y low, y high in this order; the other two coordinates lie on the surface; on every face other than the two depth faces, every depth of the surface occurs; cells may repeat. `slab_home`: block k is stored on the slab device k // 2, in its slot k % 2. `member_ids`: the members' profiles are all different.
All inputs are finite; a program needn't handle non-finite values.
Results may differ from a plain program's by a relative error of at most 0.000098.
Values sent between devices are 32-bit elements; how exact they have to be, the bound alone decides.
No kernel may reach another device: no remote copies, remote signals or barrier semaphores. Data moves between devices by JAX's collectives and lax.ppermute only.
A program may use at most 64 MiB of HBM per device.

v0:
```python
import jax
import jax.numpy as jnp
from jax import lax
from jax.sharding import PartitionSpec as P


def extended(array, sides, width):
    for axis, dim in sides:
        peers, length = (lax.axis_size(axis), array.shape[dim])
        up = [(i, (i + 1) % peers) for i in range(peers - 1)]
        down = [(j, i) for i, j in up]
        last = lax.slice_in_dim(array, length - width, length, axis=dim)
        leading = lax.slice_in_dim(array, 0, width, axis=dim)
        before = lax.ppermute(last, axis, up)
        after = lax.ppermute(leading, axis, down)
        array = jnp.concatenate([before, array, after], axis=dim)
    return array


def laplace(ext):
    inner = ext[:, 1:-1, 1:-1, :]
    beside = ext[:, 2:, 1:-1, :] + ext[:, :-2, 1:-1, :]
    beside = beside + ext[:, 1:-1, 2:, :] + ext[:, 1:-1, :-2, :]
    padded = jnp.pad(inner, ((0, 0), (0, 0), (0, 0), (1, 1)))
    beside = beside + padded[:, :, :, 2:] + padded[:, :, :, :-2]
    return beside - 6.0 * inner


def inject(field, cells, point_values, anchor_x, anchor_z, total_z):
    extent_x, extent_z, depth_y = (field.shape[1], field.shape[2], field.shape[3])
    plane = total_z * depth_y
    cell_x = cells // plane
    remain = cells % plane
    cell_z = remain // depth_y
    cell_y = remain % depth_y
    local_x = cell_x - anchor_x
    local_z = cell_z - anchor_z
    inside = (local_x >= 0) & (local_x < extent_x) & (local_z >= 0) & (local_z < extent_z)
    volume = extent_x * extent_z * depth_y
    target = jnp.where(inside, (local_x * extent_z + local_z) * depth_y + cell_y, volume)
    source = jnp.zeros((volume,), jnp.float32).at[target].add(point_values, mode="drop")
    return field + source.reshape(extent_x, extent_z, depth_y)[None]


def on_device(
    pressure_now,
    pressure_prev,
    courant_sq,
    member_profiles,
    member_ids,
    stored_slabs,
    slab_home,
    interp_weights,
    surface_cells,
):
    members, width_x, width_z, depth_y = pressure_now.shape
    total_z = width_z * lax.axis_size("slab")
    start_x = lax.axis_index("box") * width_x
    start_z = lax.axis_index("slab") * width_z
    profiles = member_profiles.shape[0]
    choose = (member_ids[:, None] == jnp.arange(profiles, dtype=jnp.int32)[None, :]).astype(
        jnp.float32
    )
    profile_all = jnp.dot(choose, member_profiles, precision=lax.Precision.HIGHEST)
    profile_here = lax.dynamic_slice_in_dim(profile_all, start_z, width_z, 1)
    coef = courant_sq[None] * (1.0 + profile_here[:, None, :, None])
    slots = stored_slabs.shape[0]
    home = slab_home[0]
    is_owner = lax.axis_index("slab") == home // slots
    mine = lax.dynamic_index_in_dim(stored_slabs, home % slots, 0, keepdims=False)
    partial_values = jnp.dot(interp_weights, mine, precision=lax.Precision.HIGHEST)
    offered = jnp.where(is_owner, partial_values, jnp.zeros_like(partial_values))
    values = lax.psum(offered, "slab")
    cells = surface_cells.reshape(-1)
    count = interp_weights.shape[0]
    prev, now = (pressure_prev, pressure_now)
    for step in range(count):
        ext = extended(now, (("box", 1), ("slab", 2)), 1)
        nxt = 2.0 * now - prev + coef * laplace(ext)
        nxt = inject(nxt, cells, values[step], start_x, start_z, total_z)
        prev, now = (now, nxt)
    return (now, prev)


def solution(mesh):
    in_specs = (
        P("ens", "box", "slab", None),
        P("ens", "box", "slab", None),
        P("box", "slab", None),
        P(),
        P("ens"),
        P("slab", None, None),
        P("ens"),
        P(),
        P(),
    )
    out_specs = (P("ens", "box", "slab", None), P("ens", "box", "slab", None))
    return jax.shard_map(
        on_device, mesh=mesh, in_specs=in_specs, out_specs=out_specs, check_vma=False
    )
```

profile of v0, /device:TPU:1, one launch (start us, length us, event | category | flops | bytes accessed | tf_op | source)
XLA Modules:
  0.0 109.3 jit_solution(6065750017297019400)
XLA Ops:
  0.6 0.0 copy-start
  0.6 0.0 copy-start.1
  0.7 0.9 fusion.31
  1.5 4.0 %collective-permute-start.1 = (f32[2,1,16,256]{3,2,1,0:T(8,128)S(1)}, f32[2,1,16,256]{3,2,1,0:T(8,128)S(1)}, u32[]{:S(2)}, u32[]{:S(2)}) collective-permute-start(f32[2,1,16,256]{3,2,1,0:T(8,128)S(1)} %get-tuple-element.9), channel_id=1, source_target_pairs={{0,4},{4,8},{8,12},{1,5},{5,9},{9,13},{2,6},{6,10},{10,14},{3,7},{... | collective-permute-start | bytes 98312 | tf_op jit(solution)/shard_map/ppermute | solution.py:14
  5.6 1.3 %collective-permute-start = (f32[2,1,16,256]{3,2,1,0:T(8,128)S(1)}, f32[2,1,16,256]{3,2,1,0:T(8,128)S(1)}, u32[]{:S(2)}, u32[]{:S(2)}) collective-permute-start(f32[2,1,16,256]{3,2,1,0:T(8,128)S(1)} %get-tuple-element.8), channel_id=1, source_target_pairs={{4,0},{8,4},{12,8},{5,1},{9,5},{13,9},{6,2},{10,6},{14,10},{7,3},{... | collective-permute-start | bytes 98312 | tf_op jit(solution)/shard_map/ppermute | solution.py:15
  7.5 0.0 copy-done
  7.5 1.0 fusion
  8.6 11.0 %psum.7 = f32[2,6144]{1,0:T(2,128)S(1)} all-reduce(f32[2,6144]{1,0:T(2,128)S(1)} %fusion), channel_id=1, replica_groups=mesh['ens'=2,'box'=4,'slab'=4] {'slab'}, use_global_device_ids=true, to_apply=%region_0.1 | all-reduce | flops 12288 | bytes 98304 | tf_op jit(solution)/shard_map/psum | solution.py:73
  19.6 0.0 copy-start.6
  19.6 0.6 fusion.32
  20.2 0.1 copy-done.6
  20.4 0.0 copy-start.8
  20.4 0.0 copy-start.9
  20.4 0.4 compare_select_fusion
  20.8 0.2 copy-done.8
  21.1 0.0 copy-done.9
  21.1 0.2 fusion.24
  21.2 0.0 collective-permute-done.1
  21.3 0.0 copy-done.1
  21.3 0.0 copy-start.4
  21.3 0.0 collective-permute-done
  21.3 0.1 fusion.29
  21.4 3.1 %collective-permute-start.2 = (f32[2,18,1,256]{3,2,1,0:T(1,128)S(1)}, f32[2,18,1,256]{3,2,1,0:T(1,128)S(1)}, u32[]{:S(2)}, u32[]{:S(2)}) collective-permute-start(f32[2,18,1,256]{3,2,1,0:T(1,128)S(1)} %get-tuple-element.4), channel_id=1, source_target_pairs={{1,0},{2,1},{3,2},{5,4},{6,5},{7,6},{9,8},{10,9},{11,10},{13,12},{... | collective-permute-start | bytes 110600 | tf_op jit(solution)/shard_map/ppermute | solution.py:15
  24.5 2.6 %collective-permute-start.3 = (f32[2,18,1,256]{3,2,1,0:T(1,128)S(1)}, f32[2,18,1,256]{3,2,1,0:T(1,128)}, u32[]{:S(2)}, u32[]{:S(2)}) collective-permute-start(f32[2,18,1,256]{3,2,1,0:T(1,128)S(1)} %get-tuple-element.5), channel_id=1, source_target_pairs={{0,1},{1,2},{2,3},{4,5},{5,6},{6,7},{8,9},{9,10},{10,11},{12,13},{... | collective-permute-start | bytes 110600 | tf_op jit(solution)/shard_map/ppermute | solution.py:14
  27.2 0.1 dynamic-slice_add_fusion
  27.2 0.0 copy-done.7
  27.2 32.6 %scatter_custom_fusion = f32[65536]{0:T(1024)S(1)} fusion(s32[6144]{0:T(1024)S(1)} %bitcast.21, f32[6144]{0:T(1024)S(1)} %bitcast.24, f32[]{:T(128)} %constant.98.clone.1), kind=kCustom, calls=%fused_computation.43 | custom fusion | flops 6144 | bytes 262148 | tf_op jit(solution)/shard_map/scatter-add | solution.py:41
  59.9 0.0 copy-start.3
  59.9 0.1 add.178
  60.0 0.0 collective-permute-done.2
  60.0 0.0 copy-start.5
  60.0 0.6 copy-done.5
  60.6 0.0 collective-permute-done.3
  60.6 0.2 copy-done.3
  60.8 1.2 %fusion.2 = f32[2,16,16,256]{3,2,1,0:T(8,128)S(1)} fusion(f32[2,16,16,256]{3,2,1,0:T(8,128)S(1)} %copy-done.1, f32[2,18,16,256]{3,2,1,0:T(8,128)S(1)} %constant_dynamic-update-slice_fusion, f32[2,18,1,256]{3,2,1,0:T(1,128)} %collective-permute-done.3, f32[2,18,1,256]{3,2,1,0:T(1,128)} %copy-done.5, f32[2,1,16,256]{3,2,1,0:T(8,128)S(1)} %collective-permute-done.1, ...), kind=kLoop, calls=%fused_computation.11 | loop fusion | flops 2228224 | bytes 2826368 | tf_op jit(solution)/shard_map/add | solution.py:42
  62.0 0.0 copy-start.2
  62.1 1.3 %collective-permute-start.4 = (f32[2,1,16,256]{3,2,1,0:T(8,128)S(1)}, f32[2,1,16,256]{3,2,1,0:T(8,128)S(1)}, u32[]{:S(2)}, u32[]{:S(2)}) collective-permute-start(f32[2,1,16,256]{3,2,1,0:T(8,128)S(1)} %get-tuple-element.7), channel_id=1, source_target_pairs={{4,0},{8,4},{12,8},{5,1},{9,5},{13,9},{6,2},{10,6},{14,10},{7,3},{... | collective-permute-start | bytes 98312 | tf_op jit(solution)/shard_map/ppermute | solution.py:15
  63.4 5.2 %collective-permute-start.5 = (f32[2,1,16,256]{3,2,1,0:T(8,128)S(1)}, f32[2,1,16,256]{3,2,1,0:T(8,128)S(1)}, u32[]{:S(2)}, u32[]{:S(2)}) collective-permute-start(f32[2,1,16,256]{3,2,1,0:T(8,128)S(1)} %get-tuple-element.6), channel_id=1, source_target_pairs={{0,4},{4,8},{8,12},{1,5},{5,9},{9,13},{2,6},{6,10},{10,14},{3,7},{... | collective-permute-start | bytes 98312 | tf_op jit(solution)/shard_map/ppermute | solution.py:14
  68.5 0.0 collective-permute-done.4
  68.5 1.0 collective-permute-done.5
  69.5 0.1 pad_maximum_fusion.14
  69.6 2.6 %collective-permute-start.6 = (f32[2,18,1,256]{3,2,1,0:T(1,128)S(1)}, f32[2,18,1,256]{3,2,1,0:T(1,128)S(1)}, u32[]{:S(2)}, u32[]{:S(2)}) collective-permute-start(f32[2,18,1,256]{3,2,1,0:T(1,128)S(1)} %get-tuple-element.2), channel_id=1, source_target_pairs={{1,0},{2,1},{3,2},{5,4},{6,5},{7,6},{9,8},{10,9},{11,10},{13,12},{... | collective-permute-start | bytes 110600 | tf_op jit(solution)/shard_map/ppermute | solution.py:15
  72.2 3.0 %collective-permute-start.7 = (f32[2,18,1,256]{3,2,1,0:T(1,128)S(1)}, f32[2,18,1,256]{3,2,1,0:T(1,128)S(1)}, u32[]{:S(2)}, u32[]{:S(2)}) collective-permute-start(f32[2,18,1,256]{3,2,1,0:T(1,128)S(1)} %get-tuple-element.3), channel_id=1, source_target_pairs={{0,1},{1,2},{2,3},{4,5},{5,6},{6,7},{8,9},{9,10},{10,11},{12,13},{... | collective-permute-start | bytes 110600 | tf_op jit(solution)/shard_map/ppermute | solution.py:14
  75.2 32.8 %scatter_custom_fusion.1 = f32[65536]{0:T(1024)S(1)} fusion(s32[6144]{0:T(1024)} %bitcast.22, f32[6144]{0:T(1024)} %bitcast.23, f32[]{:T(128)} %constant.98.clone.1), kind=kCustom, calls=%fused_computation.41 | custom fusion | flops 6144 | bytes 262656 | tf_op jit(solution)/shard_map/scatter-add | solution.py:41
  107.9 0.1 add.187
  108.0 0.0 collective-permute-done.6
  108.0 0.0 collective-permute-done.7
  108.1 1.3 %fusion.4 = f32[2,16,16,256]{3,2,1,0:T(8,128)} fusion(f32[2,16,16,256]{3,2,1,0:T(8,128)S(1)} %fusion.2, f32[2,18,1,256]{3,2,1,0:T(1,128)S(1)} %collective-permute-done.7, f32[2,1,16,256]{3,2,1,0:T(8,128)S(1)} %collective-permute-done.4, f32[2,1,16,256]{3,2,1,0:T(8,128)S(1)} %collective-permute-done.5, f32[2,18,1,256]{3,2,1,0:T(1,128)S(1)} %collective-permute-done.6, ...), kind=kLoop, calls=%fused_computation.13 | loop fusion | flops 2752512 | bytes 2236544 | tf_op jit(solution)/shard_map/add | solution.py:42
  (8 shorter events, 0.1 us)
Async XLA Ops:
  0.6 6.9 %copy-start = (f32[2,16,6144]{2,1,0:T(8,128)S(1)}, f32[2,16,6144]{2,1,0:T(8,128)}, u32[]{:S(2)}) copy-start(f32[2,16,6144]{2,1,0:T(8,128)} %param.14) | copy-start | bytes 2359300
  0.6 20.6 %copy-start.1 = (f32[2,16,16,256]{3,2,1,0:T(8,128)S(1)}, f32[2,16,16,256]{3,2,1,0:T(8,128)}, u32[]{:S(2)}) copy-start(f32[2,16,16,256]{3,2,1,0:T(8,128)} %param.9) | copy-start | bytes 1572868
  1.5 19.7 %collective-permute-start.1 = (f32[2,1,16,256]{3,2,1,0:T(8,128)S(1)}, f32[2,1,16,256]{3,2,1,0:T(8,128)S(1)}, u32[]{:S(2)}, u32[]{:S(2)}) collective-permute-start(f32[2,1,16,256]{3,2,1,0:T(8,128)S(1)} %get-tuple-element.9), channel_id=1, source_target_pairs={{0,4},{4,8},{8,12},{1,5},{5,9},{9,13},{2,6},{6,10},{10,14},{3,7},{... | collective-permute-start | bytes 98312 | tf_op jit(solution)/shard_map/ppermute | solution.py:14
  5.6 15.8 %collective-permute-start = (f32[2,1,16,256]{3,2,1,0:T(8,128)S(1)}, f32[2,1,16,256]{3,2,1,0:T(8,128)S(1)}, u32[]{:S(2)}, u32[]{:S(2)}) collective-permute-start(f32[2,1,16,256]{3,2,1,0:T(8,128)S(1)} %get-tuple-element.8), channel_id=1, source_target_pairs={{4,0},{8,4},{12,8},{5,1},{9,5},{13,9},{6,2},{10,6},{14,10},{7,3},{... | collective-permute-start | bytes 98312 | tf_op jit(solution)/shard_map/ppermute | solution.py:15
  19.6 0.8 copy-start.6
  20.4 0.7 copy-start.8
  20.4 0.7 copy-start.9
  21.1 6.2 %copy-start.7 = (s32[6144,1]{0,1:T(1,128)}, s32[6144,1]{0,1:T(1,128)S(1)}, u32[]{:S(2)}) copy-start(s32[6144,1]{0,1:T(1,128)S(1)} %compare_select_fusion) | copy-start | bytes 73732
  21.3 39.3 %copy-start.4 = (f32[2,16,16,256]{3,2,1,0:T(8,128)S(1)}, f32[2,16,16,256]{3,2,1,0:T(8,128)}, u32[]{:S(2)}) copy-start(f32[2,16,16,256]{3,2,1,0:T(8,128)} %param.10) | copy-start | bytes 1572868
  21.4 38.6 %collective-permute-start.2 = (f32[2,18,1,256]{3,2,1,0:T(1,128)S(1)}, f32[2,18,1,256]{3,2,1,0:T(1,128)S(1)}, u32[]{:S(2)}, u32[]{:S(2)}) collective-permute-start(f32[2,18,1,256]{3,2,1,0:T(1,128)S(1)} %get-tuple-element.4), channel_id=1, source_target_pairs={{1,0},{2,1},{3,2},{5,4},{6,5},{7,6},{9,8},{10,9},{11,10},{13,12},{... | collective-permute-start | bytes 110600 | tf_op jit(solution)/shard_map/ppermute | solution.py:15
  24.5 36.1 %collective-permute-start.3 = (f32[2,18,1,256]{3,2,1,0:T(1,128)S(1)}, f32[2,18,1,256]{3,2,1,0:T(1,128)}, u32[]{:S(2)}, u32[]{:S(2)}) collective-permute-start(f32[2,18,1,256]{3,2,1,0:T(1,128)S(1)} %get-tuple-element.5), channel_id=1, source_target_pairs={{0,1},{1,2},{2,3},{4,5},{5,6},{6,7},{8,9},{9,10},{10,11},{12,13},{... | collective-permute-start | bytes 110600 | tf_op jit(solution)/shard_map/ppermute | solution.py:14
  59.9 1.0 copy-start.3
  60.0 0.6 copy-start.5
  62.0 46.0 %copy-start.2 = (f32[2,16,16,256]{3,2,1,0:T(8,128)}, f32[2,16,16,256]{3,2,1,0:T(8,128)S(1)}, u32[]{:S(2)}) copy-start(f32[2,16,16,256]{3,2,1,0:T(8,128)S(1)} %fusion.2) | copy-start | bytes 1572868
  62.1 6.5 %collective-permute-start.4 = (f32[2,1,16,256]{3,2,1,0:T(8,128)S(1)}, f32[2,1,16,256]{3,2,1,0:T(8,128)S(1)}, u32[]{:S(2)}, u32[]{:S(2)}) collective-permute-start(f32[2,1,16,256]{3,2,1,0:T(8,128)S(1)} %get-tuple-element.7), channel_id=1, source_target_pairs={{4,0},{8,4},{12,8},{5,1},{9,5},{13,9},{6,2},{10,6},{14,10},{7,3},{... | collective-permute-start | bytes 98312 | tf_op jit(solution)/shard_map/ppermute | solution.py:15
  63.4 6.2 %collective-permute-start.5 = (f32[2,1,16,256]{3,2,1,0:T(8,128)S(1)}, f32[2,1,16,256]{3,2,1,0:T(8,128)S(1)}, u32[]{:S(2)}, u32[]{:S(2)}) collective-permute-start(f32[2,1,16,256]{3,2,1,0:T(8,128)S(1)} %get-tuple-element.6), channel_id=1, source_target_pairs={{0,4},{4,8},{8,12},{1,5},{5,9},{9,13},{2,6},{6,10},{10,14},{3,7},{... | collective-permute-start | bytes 98312 | tf_op jit(solution)/shard_map/ppermute | solution.py:14
  69.6 38.4 %collective-permute-start.6 = (f32[2,18,1,256]{3,2,1,0:T(1,128)S(1)}, f32[2,18,1,256]{3,2,1,0:T(1,128)S(1)}, u32[]{:S(2)}, u32[]{:S(2)}) collective-permute-start(f32[2,18,1,256]{3,2,1,0:T(1,128)S(1)} %get-tuple-element.2), channel_id=1, source_target_pairs={{1,0},{2,1},{3,2},{5,4},{6,5},{7,6},{9,8},{10,9},{11,10},{13,12},{... | collective-permute-start | bytes 110600 | tf_op jit(solution)/shard_map/ppermute | solution.py:15
  72.2 35.8 %collective-permute-start.7 = (f32[2,18,1,256]{3,2,1,0:T(1,128)S(1)}, f32[2,18,1,256]{3,2,1,0:T(1,128)S(1)}, u32[]{:S(2)}, u32[]{:S(2)}) collective-permute-start(f32[2,18,1,256]{3,2,1,0:T(1,128)S(1)} %get-tuple-element.3), channel_id=1, source_target_pairs={{0,1},{1,2},{2,3},{4,5},{5,6},{6,7},{8,9},{9,10},{10,11},{12,13},{... | collective-permute-start | bytes 110600 | tf_op jit(solution)/shard_map/ppermute | solution.py:14
where the time goes:
time: 110 us; the launch traced here: 109 us
  other arithmetic  68.5 us (62%)
  starting transfers between devices  23.1 us (21%)
  blocking collectives  11 us (10%)
  local copies, waits for them, and re-layouts  3.01 us (3%)
  between operations  1.62 us (1%)
  matrix products  1.2 us (1%)
    scatter-add x2, other arithmetic, inject(): jnp.zeros((volume,), jnp.float32).at[target].add(point_values, mode='drop')  65.4 us
    ppermute x4, starting transfers between devices, extended(): before = lax.ppermute(last, axis, up)  14.8 us
    psum x1, blocking collectives, on_device(): values = lax.psum(offered, 'slab')  11 us
    ppermute x4, starting transfers between devices, extended(): after = lax.ppermute(leading, axis, down)  8.3 us
    add x2, other arithmetic, inject(): return field + source.reshape(extent_x, extent_z, depth_y)[None]  2.5 us
  transfers between devices with their start and end apart: 8, of which 1 were waited for; matrix products, arithmetic and copies ran while one was open for 62% of the time, Pallas kernels for 0%

commit v1 on v0

--- a/solution.py
+++ b/solution.py
@@ -70,7 +70,7 @@
     mine = lax.dynamic_index_in_dim(stored_slabs, home % slots, 0, keepdims=False)
     partial_values = jnp.dot(interp_weights, mine, precision=lax.Precision.HIGHEST)
     offered = jnp.where(is_owner, partial_values, jnp.zeros_like(partial_values))
-    values = lax.psum(offered, "slab")
+    values = jnp.sum(lax.all_gather(offered, "slab"), axis=0)
     cells = surface_cells.reshape(-1)
     count = interp_weights.shape[0]
     prev, now = (pressure_prev, pressure_now)

time: 110 us -> 105 us (0.955)
  blocking collectives: 11 us -> 6.52 us
    psum x1 -> x0, blocking collectives: 11 us -> none  [on_device(): values = lax.psum(offered, 'slab')]
    all_gather x0 -> x1, blocking collectives: none -> 6.52 us  [on_device(): values = jnp.sum(lax.all_gather(offered, 'slab'), axis=0)]
    ppermute x4, starting transfers between devices: 8.3 us -> 7.06 us  [extended(): after = lax.ppermute(leading, axis, down)]
  transfers between devices with their start and end apart: 8 -> 8, of which waited for: 1 -> 1; matrix products, arithmetic and copies ran while one was open for 62% -> 64% of each run, Pallas kernels for 0% -> 0%
where the time goes in v1:
time: 105 us
  other arithmetic  68.5 us (65%)
  starting transfers between devices  22.7 us (22%)
  blocking collectives  6.52 us (6%)
  local copies, waits for them, and re-layouts  3.64 us (3%)
  between operations  1.62 us (2%)
  waiting for transfers between devices  1.19 us (1%)
    scatter-add x2, other arithmetic, inject(): jnp.zeros((volume,), jnp.float32).at[target].add(point_values, mode='drop')  65.4 us
    ppermute x4, starting transfers between devices, extended(): before = lax.ppermute(last, axis, up)  15.7 us
    ppermute x4, starting transfers between devices, extended(): after = lax.ppermute(leading, axis, down)  7.06 us
    all_gather x1, blocking collectives, on_device(): values = jnp.sum(lax.all_gather(offered, 'slab'), axis=0)  6.52 us
    add x2, other arithmetic, inject(): return field + source.reshape(extent_x, extent_z, depth_y)[None]  2.5 us
  transfers between devices with their start and end apart: 8, of which 1 were waited for; matrix products, arithmetic and copies ran while one was open for 64% of the time, Pallas kernels for 0%

profile of v1, /device:TPU:1, one launch (start us, length us, event | category | flops | bytes accessed | tf_op | source)
XLA Modules:
  0.0 104.8 jit_solution(11898029093393558072)
XLA Ops:
  0.6 0.0 copy-start
  0.6 0.9 fusion.31
  1.5 4.0 %collective-permute-start.1 = (f32[2,1,16,256]{3,2,1,0:T(8,128)S(1)}, f32[2,1,16,256]{3,2,1,0:T(8,128)S(1)}, u32[]{:S(2)}, u32[]{:S(2)}) collective-permute-start(f32[2,1,16,256]{3,2,1,0:T(8,128)S(1)} %get-tuple-element.9), channel_id=1, source_target_pairs={{0,4},{4,8},{8,12},{1,5},{5,9},{9,13},{2,6},{6,10},{10,14},{3,7},{... | collective-permute-start | bytes 98312 | tf_op jit(solution)/shard_map/ppermute | solution.py:14
  5.5 1.3 %collective-permute-start = (f32[2,1,16,256]{3,2,1,0:T(8,128)S(1)}, f32[2,1,16,256]{3,2,1,0:T(8,128)S(1)}, u32[]{:S(2)}, u32[]{:S(2)}) collective-permute-start(f32[2,1,16,256]{3,2,1,0:T(8,128)S(1)} %get-tuple-element.8), channel_id=1, source_target_pairs={{4,0},{8,4},{12,8},{5,1},{9,5},{13,9},{6,2},{10,6},{14,10},{7,3},{... | collective-permute-start | bytes 98312 | tf_op jit(solution)/shard_map/ppermute | solution.py:15
  7.5 0.0 copy-start.8
  7.5 0.0 copy-done
  7.5 0.7 copy-done.8
  8.2 0.3 fusion
  8.5 0.0 copy-start.1
  8.5 6.5 %all-gather.1 = f32[4,2,6144]{2,1,0:T(2,128)S(1)} all-gather(f32[1,2,6144]{2,1,0:T(2,128)S(1)} %fusion), channel_id=2, replica_groups=mesh['ens'=2,'box'=4,'slab'=4] {'slab'}, dimensions={0}, use_global_device_ids=true | all-gather | bytes 245760 | tf_op jit(solution)/shard_map/all_gather | solution.py:73
  15.0 0.1 reduce_sum.9
  15.1 0.0 copy-start.6
  15.1 0.6 fusion.32
  15.8 0.1 copy-done.6
  15.9 0.0 copy-start.9
  15.9 0.0 copy-start.10
  15.9 0.4 compare_select_fusion
  16.4 0.2 copy-done.9
  16.6 0.2 fusion.24
  16.8 0.0 collective-permute-done.1
  16.9 0.0 copy-start.4
  16.9 0.0 collective-permute-done
  16.9 0.1 fusion.29
  17.0 2.2 %collective-permute-start.2 = (f32[2,18,1,256]{3,2,1,0:T(1,128)S(1)}, f32[2,18,1,256]{3,2,1,0:T(1,128)S(1)}, u32[]{:S(2)}, u32[]{:S(2)}) collective-permute-start(f32[2,18,1,256]{3,2,1,0:T(1,128)S(1)} %get-tuple-element.4), channel_id=1, source_target_pairs={{1,0},{2,1},{3,2},{5,4},{6,5},{7,6},{9,8},{10,9},{11,10},{13,12},{... | collective-permute-start | bytes 110600 | tf_op jit(solution)/shard_map/ppermute | solution.py:15
  19.2 3.5 %collective-permute-start.3 = (f32[2,18,1,256]{3,2,1,0:T(1,128)S(1)}, f32[2,18,1,256]{3,2,1,0:T(1,128)}, u32[]{:S(2)}, u32[]{:S(2)}) collective-permute-start(f32[2,18,1,256]{3,2,1,0:T(1,128)S(1)} %get-tuple-element.5), channel_id=1, source_target_pairs={{0,1},{1,2},{2,3},{4,5},{5,6},{6,7},{8,9},{9,10},{10,11},{12,13},{... | collective-permute-start | bytes 110600 | tf_op jit(solution)/shard_map/ppermute | solution.py:14
  22.7 0.1 dynamic-slice_add_fusion
  22.8 32.6 %scatter_custom_fusion = f32[65536]{0:T(1024)S(1)} fusion(s32[6144]{0:T(1024)S(1)} %bitcast.23, f32[6144]{0:T(1024)S(1)} %bitcast.26, f32[]{:T(128)} %constant.99.clone.1), kind=kCustom, calls=%fused_computation.43 | custom fusion | flops 6144 | bytes 262148 | tf_op jit(solution)/shard_map/scatter-add | solution.py:41
  55.4 0.0 copy-start.3
  55.4 0.1 add.176
  55.5 0.0 collective-permute-done.2
  55.5 0.0 copy-start.5
  55.5 0.6 copy-done.5
  56.1 0.0 collective-permute-done.3
  56.1 0.2 copy-done.3
  56.3 1.2 %fusion.2 = f32[2,16,16,256]{3,2,1,0:T(8,128)S(1)} fusion(f32[2,16,16,256]{3,2,1,0:T(8,128)S(1)} %copy-done.1, f32[2,18,16,256]{3,2,1,0:T(8,128)S(1)} %constant_dynamic-update-slice_fusion, f32[2,18,1,256]{3,2,1,0:T(1,128)} %collective-permute-done.3, f32[2,18,1,256]{3,2,1,0:T(1,128)} %copy-done.5, f32[2,1,16,256]{3,2,1,0:T(8,128)S(1)} %collective-permute-done.1, ...), kind=kLoop, calls=%fused_computation.11 | loop fusion | flops 2228224 | bytes 2826368 | tf_op jit(solution)/shard_map/add | solution.py:42
  57.6 0.0 copy-start.2
  57.6 1.3 %collective-permute-start.4 = (f32[2,1,16,256]{3,2,1,0:T(8,128)S(1)}, f32[2,1,16,256]{3,2,1,0:T(8,128)S(1)}, u32[]{:S(2)}, u32[]{:S(2)}) collective-permute-start(f32[2,1,16,256]{3,2,1,0:T(8,128)S(1)} %get-tuple-element.7), channel_id=1, source_target_pairs={{4,0},{8,4},{12,8},{5,1},{9,5},{13,9},{6,2},{10,6},{14,10},{7,3},{... | collective-permute-start | bytes 98312 | tf_op jit(solution)/shard_map/ppermute | solution.py:15
  58.9 4.9 %collective-permute-start.5 = (f32[2,1,16,256]{3,2,1,0:T(8,128)S(1)}, f32[2,1,16,256]{3,2,1,0:T(8,128)S(1)}, u32[]{:S(2)}, u32[]{:S(2)}) collective-permute-start(f32[2,1,16,256]{3,2,1,0:T(8,128)S(1)} %get-tuple-element.6), channel_id=1, source_target_pairs={{0,4},{4,8},{8,12},{1,5},{5,9},{9,13},{2,6},{6,10},{10,14},{3,7},{... | collective-permute-start | bytes 98312 | tf_op jit(solution)/shard_map/ppermute | solution.py:14
  63.8 0.0 collective-permute-done.4
  63.8 1.2 %collective-permute-done.5 = f32[2,1,16,256]{3,2,1,0:T(8,128)S(1)} collective-permute-done((f32[2,1,16,256]{3,2,1,0:T(8,128)S(1)}, f32[2,1,16,256]{3,2,1,0:T(8,128)S(1)}, u32[]{:S(2)}, u32[]{:S(2)}) %collective-permute-start.5) | collective-permute-done | bytes 32800 | tf_op jit(solution)/shard_map/ppermute | solution.py:14
  65.0 0.1 pad_maximum_fusion.14
  65.0 2.3 %collective-permute-start.6 = (f32[2,18,1,256]{3,2,1,0:T(1,128)S(1)}, f32[2,18,1,256]{3,2,1,0:T(1,128)S(1)}, u32[]{:S(2)}, u32[]{:S(2)}) collective-permute-start(f32[2,18,1,256]{3,2,1,0:T(1,128)S(1)} %get-tuple-element.2), channel_id=1, source_target_pairs={{1,0},{2,1},{3,2},{5,4},{6,5},{7,6},{9,8},{10,9},{11,10},{13,12},{... | collective-permute-start | bytes 110600 | tf_op jit(solution)/shard_map/ppermute | solution.py:15
  67.3 3.3 %collective-permute-start.7 = (f32[2,18,1,256]{3,2,1,0:T(1,128)S(1)}, f32[2,18,1,256]{3,2,1,0:T(1,128)S(1)}, u32[]{:S(2)}, u32[]{:S(2)}) collective-permute-start(f32[2,18,1,256]{3,2,1,0:T(1,128)S(1)} %get-tuple-element.3), channel_id=1, source_target_pairs={{0,1},{1,2},{2,3},{4,5},{5,6},{6,7},{8,9},{9,10},{10,11},{12,13},{... | collective-permute-start | bytes 110600 | tf_op jit(solution)/shard_map/ppermute | solution.py:14
  70.6 32.8 %scatter_custom_fusion.1 = f32[65536]{0:T(1024)S(1)} fusion(s32[6144]{0:T(1024)} %bitcast.24, f32[6144]{0:T(1024)} %bitcast.25, f32[]{:T(128)} %constant.99.clone.1), kind=kCustom, calls=%fused_computation.41 | custom fusion | flops 6144 | bytes 262656 | tf_op jit(solution)/shard_map/scatter-add | solution.py:41
  103.4 0.1 add.185
  103.5 0.0 collective-permute-done.6
  103.5 0.0 collective-permute-done.7
  103.5 1.3 %fusion.4 = f32[2,16,16,256]{3,2,1,0:T(8,128)} fusion(f32[2,16,16,256]{3,2,1,0:T(8,128)S(1)} %fusion.2, f32[2,18,1,256]{3,2,1,0:T(1,128)S(1)} %collective-permute-done.7, f32[2,1,16,256]{3,2,1,0:T(8,128)S(1)} %collective-permute-done.4, f32[2,1,16,256]{3,2,1,0:T(8,128)S(1)} %collective-permute-done.5, f32[2,18,1,256]{3,2,1,0:T(1,128)S(1)} %collective-permute-done.6, ...), kind=kLoop, calls=%fused_computation.13 | loop fusion | flops 2752512 | bytes 2236544 | tf_op jit(solution)/shard_map/add | solution.py:42
  (11 shorter events, 0.1 us)
Async XLA Ops:
  0.6 6.9 %copy-start = (f32[2,16,6144]{2,1,0:T(8,128)S(1)}, f32[2,16,6144]{2,1,0:T(8,128)}, u32[]{:S(2)}) copy-start(f32[2,16,6144]{2,1,0:T(8,128)} %param.14) | copy-start | bytes 2359300
  1.5 15.3 %collective-permute-start.1 = (f32[2,1,16,256]{3,2,1,0:T(8,128)S(1)}, f32[2,1,16,256]{3,2,1,0:T(8,128)S(1)}, u32[]{:S(2)}, u32[]{:S(2)}) collective-permute-start(f32[2,1,16,256]{3,2,1,0:T(8,128)S(1)} %get-tuple-element.9), channel_id=1, source_target_pairs={{0,4},{4,8},{8,12},{1,5},{5,9},{9,13},{2,6},{6,10},{10,14},{3,7},{... | collective-permute-start | bytes 98312 | tf_op jit(solution)/shard_map/ppermute | solution.py:14
  5.5 11.4 %collective-permute-start = (f32[2,1,16,256]{3,2,1,0:T(8,128)S(1)}, f32[2,1,16,256]{3,2,1,0:T(8,128)S(1)}, u32[]{:S(2)}, u32[]{:S(2)}) collective-permute-start(f32[2,1,16,256]{3,2,1,0:T(8,128)S(1)} %get-tuple-element.8), channel_id=1, source_target_pairs={{4,0},{8,4},{12,8},{5,1},{9,5},{13,9},{6,2},{10,6},{14,10},{7,3},{... | collective-permute-start | bytes 98312 | tf_op jit(solution)/shard_map/ppermute | solution.py:15
  7.5 0.7 copy-start.8
  8.5 8.3 %copy-start.1 = (f32[2,16,16,256]{3,2,1,0:T(8,128)S(1)}, f32[2,16,16,256]{3,2,1,0:T(8,128)}, u32[]{:S(2)}) copy-start(f32[2,16,16,256]{3,2,1,0:T(8,128)} %param.9) | copy-start | bytes 1572868
  15.1 0.8 copy-start.6
  15.9 0.7 copy-start.9
  15.9 0.7 copy-start.10
  16.6 6.1 %copy-start.7 = (s32[6144,1]{0,1:T(1,128)}, s32[6144,1]{0,1:T(1,128)S(1)}, u32[]{:S(2)}) copy-start(s32[6144,1]{0,1:T(1,128)S(1)} %compare_select_fusion) | copy-start | bytes 73732
  16.9 39.3 %copy-start.4 = (f32[2,16,16,256]{3,2,1,0:T(8,128)S(1)}, f32[2,16,16,256]{3,2,1,0:T(8,128)}, u32[]{:S(2)}) copy-start(f32[2,16,16,256]{3,2,1,0:T(8,128)} %param.10) | copy-start | bytes 1572868
  17.0 38.5 %collective-permute-start.2 = (f32[2,18,1,256]{3,2,1,0:T(1,128)S(1)}, f32[2,18,1,256]{3,2,1,0:T(1,128)S(1)}, u32[]{:S(2)}, u32[]{:S(2)}) collective-permute-start(f32[2,18,1,256]{3,2,1,0:T(1,128)S(1)} %get-tuple-element.4), channel_id=1, source_target_pairs={{1,0},{2,1},{3,2},{5,4},{6,5},{7,6},{9,8},{10,9},{11,10},{13,12},{... | collective-permute-start | bytes 110600 | tf_op jit(solution)/shard_map/ppermute | solution.py:15
  19.2 36.9 %collective-permute-start.3 = (f32[2,18,1,256]{3,2,1,0:T(1,128)S(1)}, f32[2,18,1,256]{3,2,1,0:T(1,128)}, u32[]{:S(2)}, u32[]{:S(2)}) collective-permute-start(f32[2,18,1,256]{3,2,1,0:T(1,128)S(1)} %get-tuple-element.5), channel_id=1, source_target_pairs={{0,1},{1,2},{2,3},{4,5},{5,6},{6,7},{8,9},{9,10},{10,11},{12,13},{... | collective-permute-start | bytes 110600 | tf_op jit(solution)/shard_map/ppermute | solution.py:14
  55.4 1.0 copy-start.3
  55.5 0.6 copy-start.5
  57.6 45.9 %copy-start.2 = (f32[2,16,16,256]{3,2,1,0:T(8,128)}, f32[2,16,16,256]{3,2,1,0:T(8,128)S(1)}, u32[]{:S(2)}) copy-start(f32[2,16,16,256]{3,2,1,0:T(8,128)S(1)} %fusion.2) | copy-start | bytes 1572868
  57.6 6.2 %collective-permute-start.4 = (f32[2,1,16,256]{3,2,1,0:T(8,128)S(1)}, f32[2,1,16,256]{3,2,1,0:T(8,128)S(1)}, u32[]{:S(2)}, u32[]{:S(2)}) collective-permute-start(f32[2,1,16,256]{3,2,1,0:T(8,128)S(1)} %get-tuple-element.7), channel_id=1, source_target_pairs={{4,0},{8,4},{12,8},{5,1},{9,5},{13,9},{6,2},{10,6},{14,10},{7,3},{... | collective-permute-start | bytes 98312 | tf_op jit(solution)/shard_map/ppermute | solution.py:15
  58.9 6.1 %collective-permute-start.5 = (f32[2,1,16,256]{3,2,1,0:T(8,128)S(1)}, f32[2,1,16,256]{3,2,1,0:T(8,128)S(1)}, u32[]{:S(2)}, u32[]{:S(2)}) collective-permute-start(f32[2,1,16,256]{3,2,1,0:T(8,128)S(1)} %get-tuple-element.6), channel_id=1, source_target_pairs={{0,4},{4,8},{8,12},{1,5},{5,9},{9,13},{2,6},{6,10},{10,14},{3,7},{... | collective-permute-start | bytes 98312 | tf_op jit(solution)/shard_map/ppermute | solution.py:14
  65.0 38.4 %collective-permute-start.6 = (f32[2,18,1,256]{3,2,1,0:T(1,128)S(1)}, f32[2,18,1,256]{3,2,1,0:T(1,128)S(1)}, u32[]{:S(2)}, u32[]{:S(2)}) collective-permute-start(f32[2,18,1,256]{3,2,1,0:T(1,128)S(1)} %get-tuple-element.2), channel_id=1, source_target_pairs={{1,0},{2,1},{3,2},{5,4},{6,5},{7,6},{9,8},{10,9},{11,10},{13,12},{... | collective-permute-start | bytes 110600 | tf_op jit(solution)/shard_map/ppermute | solution.py:15
  67.3 36.2 %collective-permute-start.7 = (f32[2,18,1,256]{3,2,1,0:T(1,128)S(1)}, f32[2,18,1,256]{3,2,1,0:T(1,128)S(1)}, u32[]{:S(2)}, u32[]{:S(2)}) collective-permute-start(f32[2,18,1,256]{3,2,1,0:T(1,128)S(1)} %get-tuple-element.3), channel_id=1, source_target_pairs={{0,1},{1,2},{2,3},{4,5},{5,6},{6,7},{8,9},{9,10},{10,11},{12,13},{... | collective-permute-start | bytes 110600 | tf_op jit(solution)/shard_map/ppermute | solution.py:14
